TPU v7x, 32 devices: a whole 2x2x4 slice. The times are simulated.
32 devices in a mesh: grp: 4 (over z), dev: 8 (over y, x, core).
Axes of the slice: x: 2, y: 2, z: 4, core: 2. Of those that a mesh axis runs over, the one named last changes fastest.
Arguments:
- images: bfloat16 [1536, 1536], P(('grp', 'dev')), may hold values from -1 to 1, as said below
- texts: bfloat16 [1536, 1536], P(('grp', 'dev')), may hold values from -1 to 1, as said below
- logit_scale: float32 [1], replicated, may hold values from 20 to 60
- logit_bias: float32 [1], replicated, may hold values from -12 to -8
Outputs:
- grad_image: float32 [1536, 1536], P(('grp', 'dev'))
- grad_text: float32 [1536, 1536], P(('grp', 'dev'))
- loss: float32 [1], replicated
Inputs may be any that keep to these rules, and one draw needn't show every extreme that they name: `images`: every row has length 1 up to bfloat16 rounding. `texts`: every row has length 1 up to bfloat16 rounding.
All inputs are finite; a program needn't handle non-finite values.
Results may differ from a plain program's by a relative error of at most 0.00095.
Values may be sent and summed in bfloat16 or wider, within the bound.
A program may use at most 128 MiB of HBM per device.

v0:
```python
import jax
import jax.numpy as jnp
from jax import lax
from jax.sharding import PartitionSpec as P


def pair_logits(left_rows, left_ids, shard_rows, shard_ids, multiplier, offset):
    logits = (
        lax.dot_general(
            left_rows, shard_rows, (((1,), (1,)), ((), ())), preferred_element_type=jnp.float32
        )
        * multiplier
        + offset
    )
    matched = left_ids[:, None] == shard_ids[None, :]
    return (logits, matched)


def pair_weights(logits, matched):
    return (jax.nn.sigmoid(logits) - matched.astype(jnp.float32)).astype(jnp.bfloat16)


def pair_loss(logits, matched):
    labels = jnp.where(matched, 1.0, -1.0).astype(jnp.float32)
    return -jnp.sum(jax.nn.log_sigmoid(labels * logits))


def shards(images, texts, logit_scale, logit_bias):
    own_rows = images.shape[0]
    group_size = lax.axis_size("dev")
    groups = lax.axis_size("grp")
    group_index = lax.axis_index("grp")
    member = lax.axis_index("dev")
    multiplier = logit_scale[0]
    offset = logit_bias[0]
    slab_start = group_index * group_size * own_rows
    local_iota = jnp.arange(groups * own_rows, dtype=jnp.int32)
    spread_ids = (
        local_iota // own_rows * group_size * own_rows + member * own_rows + local_iota % own_rows
    )
    image_all = lax.all_gather(images, "grp", axis=0, tiled=True)
    shard_rows = lax.all_gather(texts, "dev", axis=0, tiled=True)
    shard_ids = slab_start + jnp.arange(shard_rows.shape[0], dtype=jnp.int32)
    logits, matched = pair_logits(image_all, spread_ids, shard_rows, shard_ids, multiplier, offset)
    weights = pair_weights(logits, matched)
    grad_sum = jnp.dot(weights, shard_rows, preferred_element_type=jnp.float32)
    grad_sum, weight_all, loss_sum = (grad_sum, weights, pair_loss(logits, matched))
    product = lax.dot_general(
        weight_all, image_all, (((0,), (0,)), ((), ())), preferred_element_type=jnp.float32
    )
    grad_text = lax.psum_scatter(multiplier * product, "dev", scatter_dimension=0, tiled=True)
    grad_image = lax.psum_scatter(multiplier * grad_sum, "grp", scatter_dimension=0, tiled=True)
    loss_total = lax.psum(loss_sum, ("grp", "dev"))
    batch_all = own_rows * group_size * groups
    return (grad_image, grad_text, (loss_total / batch_all).reshape(1))


def solution(mesh):
    in_specs = (P(("grp", "dev"), None), P(("grp", "dev"), None), P(), P())
    out_specs = (P(("grp", "dev"), None), P(("grp", "dev"), None), P())
    return jax.shard_map(shards, mesh=mesh, in_specs=in_specs, out_specs=out_specs, check_vma=False)
```

profile of v0, /device:TPU:0, one launch (start us, length us, event | category | flops | bytes accessed | tf_op | source)
XLA Modules:
  0.0 123.5 jit_solution(17917080121685842772)
XLA Ops:
  7.2 0.0 all-gather.2.cloned.1.call-start
  7.2 0.7 all-gather.2.cloned.1.call-update
  7.9 0.0 reduce-scatter.3.cloned.1.call-start
  9.3 18.5 %all_gather.6 = bf16[192,1536]{1,0:T(8,128)(2,1)S(1)} all-gather(bf16[48,1536]{1,0:T(8,128)(2,1)} %param.4), channel_id=1, replica_groups=mesh['grp'=4,'dev'=8] {'grp'}, dimensions={0}, use_global_device_ids=true | all-gather | bytes 737280 | tf_op jit(solution)/shard_map/all_gather | solution.py:41
  27.7 8.8 %all-gather.2.cloned.1.call-done = bf16[384,1536]{1,0:T(8,128)(2,1)} async-done(((bf16[48,1536]{1,0:T(8,128)(2,1)}), bf16[384,1536]{1,0:T(8,128)(2,1)}) %all-gather.2.cloned.1.call-update) | async-done | bytes 1179664 | tf_op jit(solution)/shard_map/all_gather | solution.py:42
  36.5 0.0 copy-start
  36.5 2.7 %fusion.5 = (f32[]{:T(128)}, f32[192,384]{1,0:T(8,128)S(1)}) fusion(s32[384]{0:T(512)S(1)} %iota_add_fusion, s32[192]{0:T(256)S(1)} %fusion.8, f32[]{:T(128)} %bitcast.10, f32[]{:T(128)} %bitcast.8, bf16[192,1536]{1,0:T(8,128)(2,1)S(1)} %all_gather.6, bf16[384,1536]{1,0:T(8,128)(2,1)} %all-gather.2.cloned.1.call-done), kind=kOutput, calls=%fused_computation.11 | convolution fusion | flops 227450880 | bytes 2066700 | tf_op jit(solution)/shard_map/dot_general | solution.py:9
  39.2 0.0 copy-done
  39.2 1.5 %convolution_multiply_fusion.1 = f32[192,1536]{1,0:T(8,128)} fusion(bf16[384,1536]{1,0:T(8,128)(2,1)S(1)} %copy-done, f32[]{:T(128)} %bitcast.7, f32[192,384]{1,0:T(8,128)S(1)} %get-tuple-element.4, s32[384]{0:T(512)S(1)} %iota_add_fusion, s32[192]{0:T(256)S(1)} %fusion.8), kind=kOutput, calls=%fused_computation.1 | convolution fusion | flops 227303424 | bytes 2656516 | tf_op jit(solution)/shard_map/dot_general | solution.py:46
  40.8 0.0 reduce-scatter.3.cloned.1.call-update
  40.8 0.0 reduce-scatter.5.cloned.1.call-start
  40.9 2.0 %convolution_multiply_fusion = f32[384,1536]{1,0:T(8,128)} fusion(bf16[192,1536]{1,0:T(8,128)(2,1)S(1)} %all_gather.6, f32[]{:T(128)} %bitcast.9, f32[192,384]{1,0:T(8,128)S(1)} %get-tuple-element.4, s32[384]{0:T(512)S(1)} %iota_add_fusion, s32[192]{0:T(256)S(1)} %fusion.8), kind=kOutput, calls=%fused_computation | convolution fusion | flops 227598336 | bytes 3246340 | tf_op jit(solution)/shard_map/dot_general | solution.py:48
  42.9 0.0 reduce-scatter.5.cloned.1.call-update
  42.9 40.7 %psum.7 = f32[]{:T(128)} all-reduce(f32[]{:T(128)} %get-tuple-element.3), channel_id=1, replica_groups=mesh['grp'=4,'dev'=8] {'grp','dev'}, use_global_device_ids=true, to_apply=%region_3.4 | all-reduce | flops 1 | bytes 8 | tf_op jit(solution)/shard_map/psum | solution.py:53
  84.3 0.0 reduce-scatter.3.cloned.1.call-done
  84.3 31.6 %reduce-scatter.5.cloned.1.call-done = f32[48,1536]{1,0:T(8,128)} async-done(((f32[384,1536]{1,0:T(8,128)}), f32[48,1536]{1,0:T(8,128)}) %reduce-scatter.5.cloned.1.call-update) | async-done | bytes 294928 | tf_op jit(solution)/shard_map/reduce_scatter | solution.py:51
  (2 shorter events, 0.0 us)
Async XLA Ops:
  7.2 29.4 %all-gather.2.cloned.1.call-start = ((), (), s32[]{:S(2)}) async-start(), calls=%async_computation.2 | async-start | bytes 1327104 | tf_op jit(solution)/shard_map/all_gather | solution.py:42
  7.9 76.4 %reduce-scatter.3.cloned.1.call-start = ((), (), s32[]{:S(2)}) async-start(), calls=%async_computation.3 | async-start | bytes 1474560 | tf_op jit(solution)/shard_map/reduce_scatter | solution.py:52
  36.5 2.7 %copy-start = (bf16[384,1536]{1,0:T(8,128)(2,1)S(1)}, bf16[384,1536]{1,0:T(8,128)(2,1)}, u32[]{:S(2)}) copy-start(bf16[384,1536]{1,0:T(8,128)(2,1)} %all-gather.2.cloned.1.call-done) | copy-start | bytes 3538948
  40.8 75.1 %reduce-scatter.5.cloned.1.call-start = ((), (), s32[]{:S(2)}) async-start(), calls=%async_computation.4 | async-start | bytes 2654208 | tf_op jit(solution)/shard_map/reduce_scatter | solution.py:51
Sparse Core Ops, SparseCore 0:
  9.9 26.6 all-gather.1
  40.9 30.0 reduce-scatter.2
  74.9 40.9 reduce-scatter.4
where the time goes:
time: 124 us
  blocking collectives  59.2 us (48%)
  waiting for transfers between devices  41.1 us (33%)
  between operations  16.8 us (14%)
  matrix products  6.25 us (5%)
    psum x1, blocking collectives, shards(): loss_total = lax.psum(loss_sum, ('grp', 'dev'))  40.7 us
    reduce_scatter x1, waiting for transfers between devices, shards(): lax.psum_scatter(multiplier * product, 'dev', scatter_dimension=0, tiled=...  31.6 us
    all_gather x1, blocking collectives, shards(): image_all = lax.all_gather(images, 'grp', axis=0, tiled=True)  18.5 us
    all_gather x1, waiting for transfers between devices, shards(): shard_rows = lax.all_gather(texts, 'dev', axis=0, tiled=True)  8.79 us
    dot_general x1, matrix products, pair_logits(): lax.dot_general(left_rows, shard_rows, (((1,), (1,)), ((), ())), preferre...  2.7 us
  transfers between devices with their start and end apart: 3, of which 2 were waited for; matrix products, arithmetic and copies ran while one was open for 2% of the time, Pallas kernels for 0%

commit v1 on v0

v1 whole, which is shorter than its diff:
```python
import functools
import math

import jax
import jax.numpy as jnp
from jax import lax
from jax.experimental import pallas as pl
from jax.experimental.pallas import tpu as pltpu
from jax.sharding import PartitionSpec as P

MESH = pl.DeviceIdType.MESH
CORES = 2


def split_chips(members):
    chips = members // CORES
    q_size = math.isqrt(chips)
    while chips % q_size:
        q_size -= 1
    return chips // q_size, q_size


def piece_count(rows):
    for pieces in (3, 2):
        if rows % (16 * pieces) == 0:
            return pieces
    return 1


def pair_terms(logits, matched):
    small = jnp.exp(-jnp.abs(logits))
    sigmoid = jnp.where(logits >= 0, 1.0, small) / (1.0 + small)
    if matched is None:
        return sigmoid, jnp.maximum(logits, 0.0) + jnp.log1p(small)
    weights = sigmoid - matched.astype(jnp.float32)
    signed = jnp.where(matched, -logits, logits)
    return weights, jnp.maximum(signed, 0.0) + jnp.log1p(small)


def kernel(
    groups, p_size, q_size, pieces,
    img_ref, txt_ref, scale_ref, bias_ref,
    gi_ref, gt_ref, loss_ref,
    img_all, txt_all, acc_i, acc_t, part_i, part_t,
    loss_acc, loss_own, loss_dev, loss_sum, loss_grp,
    img_recv, img_z, img_plane, img_core,
    txt_recv, txt_z, txt_plane, txt_core,
    pi_send, pi_recv, pt_send, pt_recv,
    ld_send, ld_recv, lg_send, lg_recv,
):
    rows = img_ref.shape[0]
    members = p_size * q_size * CORES
    g = lax.axis_index("grp")
    d = lax.axis_index("dev")
    c = lax.rem(d, CORES)
    chip = d // CORES
    q = lax.rem(chip, q_size)
    p = chip // q_size
    step_rows = rows // pieces
    multiplier = scale_ref[0]
    offset = bias_ref[0]

    def member(pi, qi, ci):
        return (pi * q_size + qi) * CORES + ci

    barrier = pltpu.get_barrier_semaphore()
    for k in range(1, members):
        pl.semaphore_signal(barrier, inc=1, device_id={"dev": lax.rem(d + k, members)}, device_id_type=MESH)
    for k in range(1, groups):
        pl.semaphore_signal(barrier, inc=1, device_id={"grp": lax.rem(g + k, groups)}, device_id_type=MESH)
    pl.semaphore_wait(barrier, members + groups - 2)

    class Side:
        def __init__(self, own, all_ref, recv, zs, ps, cs, me, size, partner):
            self.own, self.all, self.recv = own, all_ref, recv
            self.zs, self.ps, self.cs = zs, ps, cs
            self.me, self.size, self.partner = me, size, partner

        def piece(self, gg, m, cc, h):
            return self.all.at[gg, m, cc, pl.ds(h * step_rows, step_rows)]

        def copy(self, gg, m, cc, h, send, target, own=False):
            dst = self.piece(gg, m, cc, h)
            src = self.own.at[pl.ds(h * step_rows, step_rows)] if own else dst
            return pltpu.make_async_remote_copy(
                src_ref=src, dst_ref=dst, send_sem=send, recv_sem=self.recv.at[gg, m, cc, h],
                device_id=target, device_id_type=MESH,
            )

        def arrived(self, gg, m, cc, h):
            self.copy(gg, m, cc, h, self.cs.at[0, 0, 0], {"dev": member(p, q, 1 - c)}).wait_recv()

        def along_z(self, gg, h, up, own=False):
            slot = gg if (up or not own) else groups
            return self.copy(gg, self.me, c, h, self.zs.at[slot, h], {"grp": g + 1 if up else g - 1}, own)

        def to_plane(self, gg, k, h, own=False):
            other = lax.rem(self.me + k, self.size)
            return self.copy(gg, self.me, c, h, self.ps.at[gg, k - 1, h], {"dev": self.partner(other)}, own)

        def to_core(self, gg, m, h, own=False):
            return self.copy(gg, m, c, h, self.cs.at[gg, m, h], {"dev": member(p, q, 1 - c)}, own)

    texts = Side(txt_ref, txt_all, txt_recv, txt_z, txt_plane, txt_core, q, q_size, lambda o: member(p, o, c))
    images = Side(img_ref, img_all, img_recv, img_z, img_plane, img_core, p, p_size, lambda o: member(o, q, c))
    sides = (texts, images)

    def from_side(s, down):
        return (g - s, g >= s) if not down else (g + s, g + s < groups)

    for side in sides:
        for h in range(pieces):
            @pl.when(g + 1 < groups)
            def _():
                side.along_z(g, h, True, True).start()

            @pl.when(g > 0)
            def _():
                side.along_z(g, h, False, True).start()

            for k in range(1, side.size):
                side.to_plane(g, k, h, True).start()
            side.to_core(g, side.me, h, True).start()
    txt_all[g, q, c] = txt_ref[...]
    img_all[g, p, c] = img_ref[...]

    def forward_z(s):
        for side in sides:
            for h in range(pieces):
                for down in (False, True):
                    gg, there = from_side(s, down)

                    @pl.when(there)
                    def _():
                        side.arrived(gg, side.me, c, h)

                        @pl.when((g > 0) if down else (g + 1 < groups))
                        def _():
                            side.along_z(gg, h, not down).start()

                        for k in range(1, side.size):
                            side.to_plane(gg, k, h).start()
                        side.to_core(gg, side.me, h).start()

    def each_chunk(s, act):
        if s == 0:
            act(g)
            return
        for down in (False, True):
            gg, there = from_side(s, down)

            @pl.when(there)
            def _():
                act(gg)

    def relay_plane(s):
        def act(gg):
            for side in sides:
                for h in range(pieces):
                    for k in range(1, side.size):
                        other = lax.rem(side.me + k, side.size)
                        side.arrived(gg, other, c, h)
                        side.to_core(gg, other, h).start()

        each_chunk(s, act)

    def gradient(mine, other, acc, gg, first, losses):
        width = acc.shape[2]
        left = mine.all[g, :, c].reshape(mine.size * rows, width)
        right = other.all[gg].reshape(other.size * CORES * rows, width)
        logits = lax.dot_general(left, right, (((1,), (1,)), ((), ())), preferred_element_type=jnp.float32)
        logits = logits * multiplier + offset
        matched = None
        if first:
            row = lax.broadcasted_iota(jnp.int32, logits.shape, 0) - mine.me * rows
            col = lax.broadcasted_iota(jnp.int32, logits.shape, 1) - (other.me * CORES + c) * rows
            matched = (row == col) & (row >= 0) & (row < rows)
        weights, terms = pair_terms(logits, matched)
        if losses:
            loss_acc[...] = terms if first else loss_acc[...] + terms
        product = jnp.dot(weights.astype(jnp.bfloat16), right, preferred_element_type=jnp.float32)
        product = product.reshape(mine.size, rows, width)
        acc[...] = product if first else acc[...] + product

    def compute(s):
        def act(gg):
            for side in sides:
                for m in range(side.size):
                    for h in range(pieces):
                        side.arrived(gg, m, 1 - c, h)
            gradient(images, texts, acc_i, gg, s == 0, True)
            gradient(texts, images, acc_t, gg, s == 0, False)

        each_chunk(s, act)

    for s in range(groups + 2):
        if 0 < s < groups:
            forward_z(s)
        if 0 <= s - 1 < groups:
            relay_plane(s - 1)
            compute(s - 1)

    def partial(acc, part, send, recv, side, k):
        other = lax.rem(side.me + k, side.size)
        return pltpu.make_async_remote_copy(
            src_ref=acc.at[other], dst_ref=part.at[side.me], send_sem=send.at[k - 1], recv_sem=recv.at[side.me],
            device_id={"dev": side.partner(other)}, device_id_type=MESH,
        )

    def partial_in(acc, part, send, recv, side, k):
        other = lax.rem(side.me + k, side.size)
        return pltpu.make_async_remote_copy(
            src_ref=acc.at[other], dst_ref=part.at[other], send_sem=send.at[k - 1], recv_sem=recv.at[other],
            device_id={"dev": side.partner(other)}, device_id_type=MESH,
        )

    finals = ((acc_t, part_t, pt_send, pt_recv, texts, gt_ref), (acc_i, part_i, pi_send, pi_recv, images, gi_ref))
    for acc, part, send, recv, side, _ in finals:
        for k in range(1, side.size):
            partial(acc, part, send, recv, side, k).start()

    def all_sum(value, own, gathered, send, recv, axis, me, size):
        own[...] = jnp.full(own.shape, value, jnp.float32)
        gathered[me] = own[...]

        def out(k, slot):
            return pltpu.make_async_remote_copy(
                src_ref=own, dst_ref=gathered.at[slot], send_sem=send.at[k - 1], recv_sem=recv.at[slot],
                device_id={axis: lax.rem(me + k, size)}, device_id_type=MESH,
            )

        for k in range(1, size):
            out(k, me).start()
        for k in range(1, size):
            out(k, lax.rem(me + k, size)).wait_recv()
        total = gathered[0]
        for k in range(1, size):
            total = total + gathered[k]
        for k in range(1, size):
            out(k, me).wait_send()
        return total

    total = all_sum(jnp.sum(loss_acc[...]), loss_own, loss_dev, ld_send, ld_recv, "dev", d, members)
    total = all_sum(total, loss_sum, loss_grp, lg_send, lg_recv, "grp", g, groups)
    loss_ref[...] = total * (1.0 / (rows * members * groups))

    for acc, part, send, recv, side, out_ref in finals:
        total = acc[side.me]
        for k in range(1, side.size):
            partial_in(acc, part, send, recv, side, k).wait_recv()
            total = total + part[lax.rem(side.me + k, side.size)]
        out_ref[...] = multiplier * total
        for k in range(1, side.size):
            partial(acc, part, send, recv, side, k).wait_send()

    for side in sides:
        for h in range(pieces):
            @pl.when(g + 1 < groups)
            def _():
                side.along_z(g, h, True, True).wait_send()

            @pl.when(g > 0)
            def _():
                side.along_z(g, h, False, True).wait_send()

            for s in range(groups):
                def act(gg):
                    for k in range(1, side.size):
                        side.to_plane(gg, k, h).wait_send()
                    for m in range(side.size):
                        side.to_core(gg, m, h).wait_send()

                each_chunk(s, act)
                for down in (False, True):
                    if s:
                        gg, there = from_side(s, down)

                        @pl.when(there & ((g > 0) if down else (g + 1 < groups)))
                        def _():
                            side.along_z(gg, h, not down).wait_send()


def shards(groups, members, images, texts, logit_scale, logit_bias):
    rows, width = images.shape
    p_size, q_size = split_chips(members)
    pieces = piece_count(rows)
    f32, bf16 = jnp.float32, jnp.bfloat16
    dma = pltpu.SemaphoreType.DMA

    def side_sems(size):
        return [
            dma((groups, size, CORES, pieces)),
            dma((groups + 1, pieces)),
            dma((groups, max(size - 1, 1), pieces)),
            dma((groups, size, pieces)),
        ]

    vmem, smem = pl.BlockSpec(memory_space=pltpu.VMEM), pl.BlockSpec(memory_space=pltpu.SMEM)
    grad_image, grad_text, loss = pl.pallas_call(
        functools.partial(kernel, groups, p_size, q_size, pieces),
        out_shape=(
            jax.ShapeDtypeStruct((rows, width), f32),
            jax.ShapeDtypeStruct((rows, width), f32),
            jax.ShapeDtypeStruct((8, 128), f32),
        ),
        in_specs=[vmem, vmem, smem, smem],
        out_specs=(vmem, vmem, vmem),
        scratch_shapes=[
            pltpu.VMEM((groups, p_size, CORES, rows, width), bf16),
            pltpu.VMEM((groups, q_size, CORES, rows, width), bf16),
            pltpu.VMEM((p_size, rows, width), f32),
            pltpu.VMEM((q_size, rows, width), f32),
            pltpu.VMEM((p_size, rows, width), f32),
            pltpu.VMEM((q_size, rows, width), f32),
            pltpu.VMEM((p_size * rows, q_size * CORES * rows), f32),
            pltpu.VMEM((8, 128), f32),
            pltpu.VMEM((members, 8, 128), f32),
            pltpu.VMEM((8, 128), f32),
            pltpu.VMEM((groups, 8, 128), f32),
            *side_sems(p_size),
            *side_sems(q_size),
            dma((p_size,)), dma((p_size,)), dma((q_size,)), dma((q_size,)),
            dma((members,)), dma((members,)), dma((groups,)), dma((groups,)),
        ],
        compiler_params=pltpu.CompilerParams(
            collective_id=0, has_side_effects=True, vmem_limit_bytes=60 * 1024 * 1024
        ),
    )(images, texts, logit_scale, logit_bias)
    return grad_image, grad_text, loss[0, :1]


def solution(mesh):
    in_specs = (P(("grp", "dev"), None), P(("grp", "dev"), None), P(), P())
    out_specs = (P(("grp", "dev"), None), P(("grp", "dev"), None), P())
    body = functools.partial(shards, mesh.shape["grp"], mesh.shape["dev"])
    return jax.shard_map(body, mesh=mesh, in_specs=in_specs, out_specs=out_specs, check_vma=False)
```

time: 124 us -> 53.7 us (0.43)
  blocking collectives: 59.2 us -> 0 us
  Pallas kernels: 0 us -> 47.9 us
  waiting for transfers between devices: 41.1 us -> 0 us
  between operations: 16.8 us -> 1.93 us
  matrix products: 6.25 us -> 0 us
  local copies, waits for them, and re-layouts: 0.01 us -> 3.64 us
    pallas_call x0 -> x1, Pallas kernels: none -> 47.9 us  [shards(): pl.pallas_call(functools.partial(kernel, groups, p_size, q_size, pieces),...]
    psum x1 -> x0, blocking collectives: 40.7 us -> none  [shards(): loss_total = lax.psum(loss_sum, ('grp', 'dev'))]
    reduce_scatter x2 -> x0, waiting for transfers between devices: 31.6 us -> none  [the longest x1 31.6 us: shards(): lax.psum_scatter(multiplier * product, 'dev', scatter_dimension=0, tiled=...]
    all_gather x1 -> x0, blocking collectives: 18.5 us -> none  [shards(): image_all = lax.all_gather(images, 'grp', axis=0, tiled=True)]
    all_gather x1 -> x0, waiting for transfers between devices: 8.79 us -> none  [shards(): shard_rows = lax.all_gather(texts, 'dev', axis=0, tiled=True)]
    dot_general x3 -> x0, matrix products: 6.25 us -> none  [the longest x1 2.7 us: pair_logits(): lax.dot_general(left_rows, shard_rows, (((1,), (1,)), ((), ())), preferre...]
    unnamed x2 -> x4, local copies, waits for them, and re-layouts: 0.01 us -> 2.46 us
  transfers between devices with their start and end apart: 3 -> 0, of which waited for: 2 -> 0; matrix products, arithmetic and copies ran while one was open for 2% -> 0% of each run, Pallas kernels for 0% -> 0%
where the time goes in v1:
time: 53.7 us; the launch traced here: 53.5 us
  Pallas kernels  47.9 us (89%)
  local copies, waits for them, and re-layouts  3.64 us (7%)
  between operations  1.93 us (4%)
    pallas_call x1, Pallas kernels, shards(): pl.pallas_call(functools.partial(kernel, groups, p_size, q_size, pieces),...  47.9 us
    unnamed x4, local copies, waits for them, and re-layouts  2.46 us
    slice x1, local copies, waits for them, and re-layouts, shards(): return (grad_image, grad_text, loss[0, :1])  1.18 us

profile of v1, /device:TPU:0, one launch (start us, length us, event | category | flops | bytes accessed | tf_op | source)
XLA Modules:
  0.0 53.5 jit_solution(11437146759477493676)
XLA Ops:
  1.9 47.9 %shard_map.67 = (f32[48,1536]{1,0:T(8,128)}, f32[48,1536]{1,0:T(8,128)}, f32[8,128]{1,0:T(8,128)}) custom-call(bf16[48,1536]{1,0:T(8,128)(2,1)} %img_ref.1, bf16[48,1536]{1,0:T(8,128)(2,1)} %txt_ref.1, f32[1]{0:T(128)S(6)} %copy.9.scale_ref, f32[1]{0:T(128)S(6)} %copy.10.bias_ref), custom_call_target="tpu_custom_call" | custom-call | tf_op jit(solution)/shard_map/pallas_call | solution.py:299
  49.8 1.2 %slice.3 = f32[1,1]{1,0:T(1,128)} slice(f32[8,128]{1,0:T(8,128)} %get-tuple-element.8), slice={[0:1], [0:1]} | slice | bytes 8 | tf_op jit(solution)/shard_map/slice | solution.py:329
  51.0 0.0 copy-start
  51.0 1.7 %copy.11 = f32[48,1536]{1,0:T(8,128)} copy(f32[48,1536]{1,0:T(8,128)} %get-tuple-element.12) | data formatting | bytes 589824
  52.7 0.0 copy-done
  52.7 0.7 %copy.12 = f32[48,1536]{1,0:T(8,128)} copy(f32[48,1536]{1,0:T(8,128)S(1)} %copy-done) | data formatting | bytes 589824
Async XLA Ops:
  51.0 1.7 %copy-start = (f32[48,1536]{1,0:T(8,128)S(1)}, f32[48,1536]{1,0:T(8,128)}, u32[]{:S(2)}) copy-start(f32[48,1536]{1,0:T(8,128)} %get-tuple-element.13) | copy-start | bytes 884740

commit v2 on v1

v2 whole, which is shorter than its diff:
```python
import functools
import math

import jax
import jax.numpy as jnp
from jax import lax
from jax.experimental import pallas as pl
from jax.experimental.pallas import tpu as pltpu
from jax.sharding import PartitionSpec as P

MESH = pl.DeviceIdType.MESH
CORES = 2


def split_chips(members):
    chips = members // CORES
    q_size = math.isqrt(chips)
    while chips % q_size:
        q_size -= 1
    return chips // q_size, q_size


def piece_count(rows):
    for pieces in (3, 2):
        if rows % (16 * pieces) == 0:
            return pieces
    return 1


def pair_terms(logits, matched):
    small = jnp.exp(-jnp.abs(logits))
    sigmoid = jnp.where(logits >= 0, 1.0, small) / (1.0 + small)
    if matched is None:
        return sigmoid, jnp.maximum(logits, 0.0) + jnp.log1p(small)
    weights = sigmoid - matched.astype(jnp.float32)
    signed = jnp.where(matched, -logits, logits)
    return weights, jnp.maximum(signed, 0.0) + jnp.log1p(small)


def kernel(
    groups, p_size, q_size, pieces,
    img_hbm, txt_hbm, scale_hbm, bias_hbm,
    gi_ref, gt_ref, loss_ref,
    img_all, txt_all, acc_i, acc_t, part_i, part_t,
    loss_acc, loss_own, loss_dev, loss_sum, loss_grp,
    img_recv, img_z, img_plane, img_core,
    txt_recv, txt_z, txt_plane, txt_core,
    pi_send, pi_recv, pt_send, pt_recv,
    ld_send, ld_recv, lg_send, lg_recv,
    scale_ref, bias_ref, fetch_sem,
):
    rows = img_hbm.shape[0]
    members = p_size * q_size * CORES
    g = lax.axis_index("grp")
    d = lax.axis_index("dev")
    c = lax.rem(d, CORES)
    chip = d // CORES
    q = lax.rem(chip, q_size)
    p = chip // q_size
    step_rows = rows // pieces

    def member(pi, qi, ci):
        return (pi * q_size + qi) * CORES + ci

    fetches = [
        pltpu.make_async_copy(src, dst, fetch_sem.at[i])
        for i, (src, dst) in enumerate((
            (txt_hbm, txt_all.at[g, q, c]), (img_hbm, img_all.at[g, p, c]), (scale_hbm, scale_ref), (bias_hbm, bias_ref),
        ))
    ]
    barrier = pltpu.get_barrier_semaphore()

    def greet(axis, index):
        pl.semaphore_signal(barrier, inc=1, device_id={axis: index}, device_id_type=MESH)

    @pl.when(g + 1 < groups)
    def _():
        greet("grp", g + 1)

    @pl.when(g > 0)
    def _():
        greet("grp", g - 1)

    for k in range(1, p_size):
        greet("dev", member(lax.rem(p + k, p_size), q, c))
    for k in range(1, q_size):
        greet("dev", member(p, lax.rem(q + k, q_size), c))
    greet("dev", member(p, q, 1 - c))
    for fetch in fetches:
        fetch.start()
    edges = (g > 0).astype(jnp.int32) + (g + 1 < groups).astype(jnp.int32)
    pl.semaphore_wait(barrier, p_size + q_size - 1 + edges)

    class Side:
        def __init__(self, all_ref, recv, zs, ps, cs, me, size, partner):
            self.all, self.recv = all_ref, recv
            self.zs, self.ps, self.cs = zs, ps, cs
            self.me, self.size, self.partner = me, size, partner

        def piece(self, gg, m, cc, h):
            return self.all.at[gg, m, cc, pl.ds(h * step_rows, step_rows)]

        def copy(self, gg, m, cc, h, send, target):
            dst = self.piece(gg, m, cc, h)
            return pltpu.make_async_remote_copy(
                src_ref=dst, dst_ref=dst, send_sem=send, recv_sem=self.recv.at[gg, m, cc, h],
                device_id=target, device_id_type=MESH,
            )

        def arrived(self, gg, m, cc, h):
            self.copy(gg, m, cc, h, self.cs.at[0, 0, 0], {"dev": member(p, q, 1 - c)}).wait_recv()

        def along_z(self, gg, h, up, own=False):
            slot = gg if (up or not own) else groups
            return self.copy(gg, self.me, c, h, self.zs.at[slot, h], {"grp": g + 1 if up else g - 1})

        def to_plane(self, gg, k, h):
            other = lax.rem(self.me + k, self.size)
            return self.copy(gg, self.me, c, h, self.ps.at[gg, k - 1, h], {"dev": self.partner(other)})

        def to_core(self, gg, m, h):
            return self.copy(gg, m, c, h, self.cs.at[gg, m, h], {"dev": member(p, q, 1 - c)})

    texts = Side(txt_all, txt_recv, txt_z, txt_plane, txt_core, q, q_size, lambda o: member(p, o, c))
    images = Side(img_all, img_recv, img_z, img_plane, img_core, p, p_size, lambda o: member(o, q, c))
    sides = (texts, images)

    def from_side(s, down):
        return (g - s, g >= s) if not down else (g + s, g + s < groups)

    for side, fetch in zip(sides, fetches):
        fetch.wait()
        for h in range(pieces):
            @pl.when(g + 1 < groups)
            def _():
                side.along_z(g, h, True, True).start()

            @pl.when(g > 0)
            def _():
                side.along_z(g, h, False, True).start()

            for k in range(1, side.size):
                side.to_plane(g, k, h).start()
            side.to_core(g, side.me, h).start()
    for fetch in fetches[2:]:
        fetch.wait()
    multiplier = scale_ref[0]
    offset = bias_ref[0]

    def forward_z(s, side):
        for h in range(pieces):
            for down in (False, True):
                gg, there = from_side(s, down)

                @pl.when(there)
                def _():
                    side.arrived(gg, side.me, c, h)

                    @pl.when((g > 0) if down else (g + 1 < groups))
                    def _():
                        side.along_z(gg, h, not down).start()

                    for k in range(1, side.size):
                        side.to_plane(gg, k, h).start()
                    side.to_core(gg, side.me, h).start()

    def each_chunk(s, act):
        if s == 0:
            act(g)
            return
        for down in (False, True):
            gg, there = from_side(s, down)

            @pl.when(there)
            def _():
                act(gg)

    def relay_plane(s, side):
        def act(gg):
            for h in range(pieces):
                for k in range(1, side.size):
                    other = lax.rem(side.me + k, side.size)
                    side.arrived(gg, other, c, h)
                    side.to_core(gg, other, h).start()

        each_chunk(s, act)

    def gradient(mine, other, acc, gg, first, losses):
        width = acc.shape[2]
        left = mine.all[g, :, c].reshape(mine.size * rows, width)
        right = other.all[gg].reshape(other.size * CORES * rows, width)
        logits = lax.dot_general(left, right, (((1,), (1,)), ((), ())), preferred_element_type=jnp.float32)
        logits = logits * multiplier + offset
        matched = None
        if first:
            row = lax.broadcasted_iota(jnp.int32, logits.shape, 0) - mine.me * rows
            col = lax.broadcasted_iota(jnp.int32, logits.shape, 1) - (other.me * CORES + c) * rows
            matched = (row == col) & (row >= 0) & (row < rows)
        weights, terms = pair_terms(logits, matched)
        if losses:
            loss_acc[...] = terms if first else loss_acc[...] + terms
        product = jnp.dot(weights.astype(jnp.bfloat16), right, preferred_element_type=jnp.float32)
        product = product.reshape(mine.size, rows, width)
        acc[...] = product if first else acc[...] + product

    def compute(s, mine, other, acc, losses):
        def act(gg):
            for m in range(other.size):
                for h in range(pieces):
                    other.arrived(gg, m, 1 - c, h)
            gradient(mine, other, acc, gg, s == 0, losses)

        each_chunk(s, act)

    def partial(acc, part, send, recv, side, k):
        other = lax.rem(side.me + k, side.size)
        return pltpu.make_async_remote_copy(
            src_ref=acc.at[other], dst_ref=part.at[side.me], send_sem=send.at[k - 1], recv_sem=recv.at[side.me],
            device_id={"dev": side.partner(other)}, device_id_type=MESH,
        )

    def partial_in(acc, part, send, recv, side, k):
        other = lax.rem(side.me + k, side.size)
        return pltpu.make_async_remote_copy(
            src_ref=acc.at[other], dst_ref=part.at[other], send_sem=send.at[k - 1], recv_sem=recv.at[other],
            device_id={"dev": side.partner(other)}, device_id_type=MESH,
        )

    def send_partials(acc, part, send, recv, side):
        for k in range(1, side.size):
            partial(acc, part, send, recv, side, k).start()

    def loss_copy(own, gathered, send, recv, axis, me, size, k, slot):
        return pltpu.make_async_remote_copy(
            src_ref=own, dst_ref=gathered.at[slot], send_sem=send.at[k - 1], recv_sem=recv.at[slot],
            device_id={axis: lax.rem(me + k, size)}, device_id_type=MESH,
        )

    def loss_out(value, own, gathered, send, recv, axis, me, size):
        own[...] = value
        gathered[me] = value
        for k in range(1, size):
            loss_copy(own, gathered, send, recv, axis, me, size, k, me).start()

    def loss_in(own, gathered, send, recv, axis, me, size):
        for k in range(1, size):
            loss_copy(own, gathered, send, recv, axis, me, size, k, lax.rem(me + k, size)).wait_recv()
        total = gathered[0]
        for k in range(1, size):
            total = total + gathered[k]
        return total

    over_dev = (loss_own, loss_dev, ld_send, ld_recv, "dev", d, members)
    over_grp = (loss_sum, loss_grp, lg_send, lg_recv, "grp", g, groups)
    text_part = (acc_t, part_t, pt_send, pt_recv, texts)
    image_part = (acc_i, part_i, pi_send, pi_recv, images)

    last = groups - 1
    for s in range(groups):
        if s:
            forward_z(s, texts)
            if s > 1:
                relay_plane(s - 1, images)
            compute(s - 1, texts, images, acc_t, False)
            forward_z(s, images)
        relay_plane(s, texts)
        if s == 0:
            relay_plane(s, images)
        compute(s, images, texts, acc_i, True)
    loss_out(jnp.full((8, 128), jnp.sum(loss_acc[...]), jnp.float32), *over_dev)
    send_partials(*image_part)
    if last:
        relay_plane(last, images)
    compute(last, texts, images, acc_t, False)
    send_partials(*text_part)
    loss_out(loss_in(*over_dev), *over_grp)
    loss_ref[...] = loss_in(*over_grp) * (1.0 / (rows * members * groups))

    for (acc, part, send, recv, side), out_ref in ((image_part, gi_ref), (text_part, gt_ref)):
        total = acc[side.me]
        for k in range(1, side.size):
            partial_in(acc, part, send, recv, side, k).wait_recv()
            total = total + part[lax.rem(side.me + k, side.size)]
        out_ref[...] = multiplier * total
        for k in range(1, side.size):
            partial(acc, part, send, recv, side, k).wait_send()
    for own, gathered, send, recv, axis, me, size in (over_dev, over_grp):
        for k in range(1, size):
            loss_copy(own, gathered, send, recv, axis, me, size, k, me).wait_send()

    for side in sides:
        for h in range(pieces):
            @pl.when(g + 1 < groups)
            def _():
                side.along_z(g, h, True, True).wait_send()

            @pl.when(g > 0)
            def _():
                side.along_z(g, h, False, True).wait_send()

            for s in range(groups):
                def act(gg):
                    for k in range(1, side.size):
                        side.to_plane(gg, k, h).wait_send()
                    for m in range(side.size):
                        side.to_core(gg, m, h).wait_send()

                each_chunk(s, act)
                for down in (False, True):
                    if s:
                        gg, there = from_side(s, down)

                        @pl.when(there & ((g > 0) if down else (g + 1 < groups)))
                        def _():
                            side.along_z(gg, h, not down).wait_send()


def write_out(gi_ref, gt_ref, loss_ref, gi_out, gt_out, loss_out):
    gi_out[...] = gi_ref[...]
    gt_out[...] = gt_ref[...]
    loss_out[0] = jnp.max(loss_ref[...])


def shards(groups, members, images, texts, logit_scale, logit_bias):
    rows, width = images.shape
    p_size, q_size = split_chips(members)
    pieces = piece_count(rows)
    f32, bf16 = jnp.float32, jnp.bfloat16
    dma = pltpu.SemaphoreType.DMA

    def side_sems(size):
        return [
            dma((groups, size, CORES, pieces)),
            dma((groups + 1, pieces)),
            dma((groups, max(size - 1, 1), pieces)),
            dma((groups, size, pieces)),
        ]

    held = (groups * (p_size + q_size) * CORES * 2 + (p_size + q_size) * 8) * rows * width
    vmem, smem = pl.BlockSpec(memory_space=pltpu.VMEM), pl.BlockSpec(memory_space=pltpu.SMEM)
    grad_image, grad_text, loss = pl.pallas_call(
        functools.partial(kernel, groups, p_size, q_size, pieces),
        out_shape=(
            jax.ShapeDtypeStruct((rows, width), f32),
            jax.ShapeDtypeStruct((rows, width), f32),
            jax.ShapeDtypeStruct((8, 128), f32),
        ),
        in_specs=[pl.BlockSpec(memory_space=pl.ANY)] * 4,
        out_specs=(vmem, vmem, vmem),
        scratch_shapes=[
            pltpu.VMEM((groups, p_size, CORES, rows, width), bf16),
            pltpu.VMEM((groups, q_size, CORES, rows, width), bf16),
            pltpu.VMEM((p_size, rows, width), f32),
            pltpu.VMEM((q_size, rows, width), f32),
            pltpu.VMEM((p_size, rows, width), f32),
            pltpu.VMEM((q_size, rows, width), f32),
            pltpu.VMEM((p_size * rows, q_size * CORES * rows), f32),
            pltpu.VMEM((8, 128), f32),
            pltpu.VMEM((members, 8, 128), f32),
            pltpu.VMEM((8, 128), f32),
            pltpu.VMEM((groups, 8, 128), f32),
            *side_sems(p_size),
            *side_sems(q_size),
            dma((p_size,)), dma((p_size,)), dma((q_size,)), dma((q_size,)),
            dma((members,)), dma((members,)), dma((groups,)), dma((groups,)),
            pltpu.SMEM((1,), f32), pltpu.SMEM((1,), f32), dma((4,)),
        ],
        compiler_params=pltpu.CompilerParams(
            collective_id=0, has_side_effects=True, vmem_limit_bytes=min(held + (members + groups) * 4096 + (12 << 20), 60 << 20)
        ),
    )(images, texts, logit_scale, logit_bias)
    return pl.pallas_call(
        write_out,
        out_shape=(
            jax.ShapeDtypeStruct((rows, width), f32),
            jax.ShapeDtypeStruct((rows, width), f32),
            jax.ShapeDtypeStruct((1,), f32),
        ),
        in_specs=[vmem, vmem, vmem],
        out_specs=(vmem, vmem, smem),
        compiler_params=pltpu.CompilerParams(vmem_limit_bytes=4 << 20),
    )(grad_image, grad_text, loss)


def solution(mesh):
    in_specs = (P(("grp", "dev"), None), P(("grp", "dev"), None), P(), P())
    out_specs = (P(("grp", "dev"), None), P(("grp", "dev"), None), P())
    body = functools.partial(shards, mesh.shape["grp"], mesh.shape["dev"])
    return jax.shard_map(body, mesh=mesh, in_specs=in_specs, out_specs=out_specs, check_vma=False)
```

time: 53.7 us -> 49.4 us (0.920)
  Pallas kernels: 47.9 us -> 45.5 us
  local copies, waits for them, and re-layouts: 3.64 us -> 1.81 us
    pallas_call x1, Pallas kernels: 47.9 us -> 44.6 us  [shards(): pl.pallas_call(functools.partial(kernel, groups, p_size, q_size, pieces),...]
    slice x1 -> x0, local copies, waits for them, and re-layouts: 1.18 us -> none  [shards(): return (grad_image, grad_text, loss[0, :1])]
    pallas_call x0 -> x1, Pallas kernels: none -> 0.84 us  [shards(): pl.pallas_call(write_out, out_shape=(jax.ShapeDtypeStruct((rows, width),...]
    unnamed x4, local copies, waits for them, and re-layouts: 2.46 us -> 1.81 us
where the time goes in v2:
time: 49.4 us; the launch traced here: 49.2 us
  Pallas kernels  45.5 us (92%)
  between operations  1.94 us (4%)
  local copies, waits for them, and re-layouts  1.81 us (4%)
    pallas_call x1, Pallas kernels, shards(): pl.pallas_call(functools.partial(kernel, groups, p_size, q_size, pieces),...  44.6 us
    unnamed x4, local copies, waits for them, and re-layouts  1.81 us

profile of v2, /device:TPU:0, one launch (start us, length us, event | category | flops | bytes accessed | tf_op | source)
XLA Modules:
  0.0 49.2 jit_solution(13569226172728214544)
XLA Ops:
  1.9 0.0 copy-start
  1.9 0.9 %copy-done = bf16[48,1536]{1,0:T(8,128)(2,1)S(1)} copy-done((bf16[48,1536]{1,0:T(8,128)(2,1)S(1)}, bf16[48,1536]{1,0:T(8,128)(2,1)}, u32[]{:S(2)}) %copy-start) | copy-done | bytes 147480
  2.8 0.0 copy-start.1
  2.8 0.9 %copy-done.1 = bf16[48,1536]{1,0:T(8,128)(2,1)S(1)} copy-done((bf16[48,1536]{1,0:T(8,128)(2,1)S(1)}, bf16[48,1536]{1,0:T(8,128)(2,1)}, u32[]{:S(2)}) %copy-start.1) | copy-done | bytes 147480
  3.7 44.6 %shard_map.67 = (f32[48,1536]{1,0:T(8,128)S(1)}, f32[48,1536]{1,0:T(8,128)S(1)}, f32[8,128]{1,0:T(8,128)S(1)}) custom-call(bf16[48,1536]{1,0:T(8,128)(2,1)S(1)} %copy-done, bf16[48,1536]{1,0:T(8,128)(2,1)S(1)} %copy-done.1, f32[1]{0:T(128)S(6)} %copy.7.scale_hbm, f32[1]{0:T(128)S(6)} %copy.8.bias_hbm), custom_call_target="tpu_custom_call" | custom-call | tf_op jit(solution)/shard_map/pallas_call | solution.py:341
  48.4 0.8 %shard_map.68 = (f32[48,1536]{1,0:T(8,128)}, f32[48,1536]{1,0:T(8,128)}, f32[1]{0:T(128)}) custom-call(f32[48,1536]{1,0:T(8,128)S(1)} %get-tuple-element.6.gi_ref, f32[48,1536]{1,0:T(8,128)S(1)} %get-tuple-element.7.gt_ref, f32[8,128]{1,0:T(8,128)S(1)} %get-tuple-element.8.loss_ref), custom_call_target="tpu_custom_call" | custom-call | tf_op jit(solution)/shard_map/pallas_call | solution.py:372
Async XLA Ops:
  1.9 0.9 %copy-start = (bf16[48,1536]{1,0:T(8,128)(2,1)S(1)}, bf16[48,1536]{1,0:T(8,128)(2,1)}, u32[]{:S(2)}) copy-start(bf16[48,1536]{1,0:T(8,128)(2,1)} %img_hbm.1) | copy-start | bytes 442372
  2.8 0.9 %copy-start.1 = (bf16[48,1536]{1,0:T(8,128)(2,1)S(1)}, bf16[48,1536]{1,0:T(8,128)(2,1)}, u32[]{:S(2)}) copy-start(bf16[48,1536]{1,0:T(8,128)(2,1)} %txt_hbm.1) | copy-start | bytes 442372

commit v3 on v2

--- a/solution.py
+++ b/solution.py
@@ -256,21 +256,18 @@
     image_part = (acc_i, part_i, pi_send, pi_recv, images)
 
     last = groups - 1
-    for s in range(groups):
-        if s:
-            forward_z(s, texts)
-            if s > 1:
-                relay_plane(s - 1, images)
-            compute(s - 1, texts, images, acc_t, False)
-            forward_z(s, images)
-        relay_plane(s, texts)
-        if s == 0:
-            relay_plane(s, images)
-        compute(s, images, texts, acc_i, True)
+    for s in range(1, groups):
+        forward_z(s, texts)
+        forward_z(s, images)
+        relay_plane(s - 1, texts)
+        relay_plane(s - 1, images)
+        compute(s - 1, images, texts, acc_i, True)
+        compute(s - 1, texts, images, acc_t, False)
+    relay_plane(last, texts)
+    relay_plane(last, images)
+    compute(last, images, texts, acc_i, True)
     loss_out(jnp.full((8, 128), jnp.sum(loss_acc[...]), jnp.float32), *over_dev)
     send_partials(*image_part)
-    if last:
-        relay_plane(last, images)
     compute(last, texts, images, acc_t, False)
     send_partials(*text_part)
     loss_out(loss_in(*over_dev), *over_grp)

time: 49.4 us -> 45.4 us (0.919)
  Pallas kernels: 45.5 us -> 41.5 us
    pallas_call x1, Pallas kernels: 44.6 us -> 40.6 us  [shards(): pl.pallas_call(functools.partial(kernel, groups, p_size, q_size, pieces),...]
where the time goes in v3:
time: 45.4 us; the launch traced here: 45.2 us
  Pallas kernels  41.5 us (91%)
  between operations  1.94 us (4%)
  local copies, waits for them, and re-layouts  1.81 us (4%)
    pallas_call x1, Pallas kernels, shards(): pl.pallas_call(functools.partial(kernel, groups, p_size, q_size, pieces),...  40.6 us
    unnamed x4, local copies, waits for them, and re-layouts  1.81 us

profile of v3, /device:TPU:0, one launch (start us, length us, event | category | flops | bytes accessed | tf_op | source)
XLA Modules:
  0.0 45.2 jit_solution(12621221081407592282)
XLA Ops:
  1.9 0.0 copy-start
  1.9 0.9 %copy-done = bf16[48,1536]{1,0:T(8,128)(2,1)S(1)} copy-done((bf16[48,1536]{1,0:T(8,128)(2,1)S(1)}, bf16[48,1536]{1,0:T(8,128)(2,1)}, u32[]{:S(2)}) %copy-start) | copy-done | bytes 147480
  2.8 0.0 copy-start.1
  2.8 0.9 %copy-done.1 = bf16[48,1536]{1,0:T(8,128)(2,1)S(1)} copy-done((bf16[48,1536]{1,0:T(8,128)(2,1)S(1)}, bf16[48,1536]{1,0:T(8,128)(2,1)}, u32[]{:S(2)}) %copy-start.1) | copy-done | bytes 147480
  3.7 40.6 %shard_map.67 = (f32[48,1536]{1,0:T(8,128)S(1)}, f32[48,1536]{1,0:T(8,128)S(1)}, f32[8,128]{1,0:T(8,128)S(1)}) custom-call(bf16[48,1536]{1,0:T(8,128)(2,1)S(1)} %copy-done, bf16[48,1536]{1,0:T(8,128)(2,1)S(1)} %copy-done.1, f32[1]{0:T(128)S(6)} %copy.7.scale_hbm, f32[1]{0:T(128)S(6)} %copy.8.bias_hbm), custom_call_target="tpu_custom_call" | custom-call | tf_op jit(solution)/shard_map/pallas_call | solution.py:338
  44.4 0.8 %shard_map.68 = (f32[48,1536]{1,0:T(8,128)}, f32[48,1536]{1,0:T(8,128)}, f32[1]{0:T(128)}) custom-call(f32[48,1536]{1,0:T(8,128)S(1)} %get-tuple-element.6.gi_ref, f32[48,1536]{1,0:T(8,128)S(1)} %get-tuple-element.7.gt_ref, f32[8,128]{1,0:T(8,128)S(1)} %get-tuple-element.8.loss_ref), custom_call_target="tpu_custom_call" | custom-call | tf_op jit(solution)/shard_map/pallas_call | solution.py:369
Async XLA Ops:
  1.9 0.9 %copy-start = (bf16[48,1536]{1,0:T(8,128)(2,1)S(1)}, bf16[48,1536]{1,0:T(8,128)(2,1)}, u32[]{:S(2)}) copy-start(bf16[48,1536]{1,0:T(8,128)(2,1)} %img_hbm.1) | copy-start | bytes 442372
  2.8 0.9 %copy-start.1 = (bf16[48,1536]{1,0:T(8,128)(2,1)S(1)}, bf16[48,1536]{1,0:T(8,128)(2,1)}, u32[]{:S(2)}) copy-start(bf16[48,1536]{1,0:T(8,128)(2,1)} %txt_hbm.1) | copy-start | bytes 442372

commit v4 on v3

--- a/solution.py
+++ b/solution.py
@@ -365,7 +365,7 @@
         compiler_params=pltpu.CompilerParams(
             collective_id=0, has_side_effects=True, vmem_limit_bytes=min(held + (members + groups) * 4096 + (12 << 20), 60 << 20)
         ),
-    )(images, texts, logit_scale, logit_bias)
+    )(pltpu.with_memory_space_constraint(images, pltpu.HBM), pltpu.with_memory_space_constraint(texts, pltpu.HBM), logit_scale, logit_bias)
     return pl.pallas_call(
         write_out,
         out_shape=(

time: 45.4 us -> 43.6 us (0.960)
  local copies, waits for them, and re-layouts: 1.81 us -> 0 us
    unnamed x4 -> x0, local copies, waits for them, and re-layouts: 1.81 us -> none
where the time goes in v4:
time: 43.6 us; the launch traced here: 43.5 us
  Pallas kernels  41.5 us (95%)
  between operations  1.93 us (4%)
    pallas_call x1, Pallas kernels, shards(): pl.pallas_call(functools.partial(kernel, groups, p_size, q_size, pieces),...  40.7 us

profile of v4, /device:TPU:0, one launch (start us, length us, event | category | flops | bytes accessed | tf_op | source)
XLA Modules:
  0.0 43.5 jit_solution(2492184468159872502)
XLA Ops:
  1.9 40.7 %shard_map.67 = (f32[48,1536]{1,0:T(8,128)S(1)}, f32[48,1536]{1,0:T(8,128)S(1)}, f32[8,128]{1,0:T(8,128)S(1)}) custom-call(bf16[48,1536]{1,0:T(8,128)(2,1)} %img_hbm.1, bf16[48,1536]{1,0:T(8,128)(2,1)} %txt_hbm.1, f32[1]{0:T(128)S(6)} %copy.7.scale_hbm, f32[1]{0:T(128)S(6)} %copy.8.bias_hbm), custom_call_target="tpu_custom_call" | custom-call | tf_op jit(solution)/shard_map/pallas_call | solution.py:338
  42.6 0.8 %shard_map.68 = (f32[48,1536]{1,0:T(8,128)}, f32[48,1536]{1,0:T(8,128)}, f32[1]{0:T(128)}) custom-call(f32[48,1536]{1,0:T(8,128)S(1)} %get-tuple-element.6.gi_ref, f32[48,1536]{1,0:T(8,128)S(1)} %get-tuple-element.7.gt_ref, f32[8,128]{1,0:T(8,128)S(1)} %get-tuple-element.8.loss_ref), custom_call_target="tpu_custom_call" | custom-call | tf_op jit(solution)/shard_map/pallas_call | solution.py:369
